TPU v7x, 128 devices: a whole 4x4x4 slice. The times are simulated.
128 devices in a mesh: dp: 1, tp: 2 (over core), cp: 64 (over z, y, x).
Axes of the slice: x: 4, y: 4, z: 4, core: 2. Of those that a mesh axis runs over, the one named last changes fastest.
Arguments:
- hidden_in: bfloat16 [8192, 1536], P(('dp', 'cp', 'tp'))
- positions: int32 [8192], P(('dp', 'cp', 'tp'))
- cache_len: int32 [1], P('dp')
- cache_k: bfloat16 [32768, 256], P(('dp', 'cp', 'tp'))
- cache_v: bfloat16 [32768, 256], P(('dp', 'cp', 'tp'))
- norm1_gain: bfloat16 [1536], replicated
- w_query: bfloat16 [1536, 1536], P(None, 'tp')
- w_key: bfloat16 [1536, 256], P(None, 'tp')
- w_value: bfloat16 [1536, 256], P(None, 'tp')
- w_out: bfloat16 [1536, 1536], P('tp')
- norm2_gain: bfloat16 [1536], replicated
- w_gate: bfloat16 [1536, 8960], P(None, 'tp')
- w_up: bfloat16 [1536, 8960], P(None, 'tp')
- w_down: bfloat16 [8960, 1536], P('tp')
Outputs:
- output: bfloat16 [8192, 1536], P(('dp', 'cp', 'tp'))
All inputs are finite; a program needn't handle non-finite values.
Results may differ from a plain program's by a relative error of at most 0.011224.
Values are sent between devices in bfloat16 or wider.
A program may use at most 1 GiB of HBM per device.

v0:
```python
import math
import jax
import jax.numpy as jnp
from jax import lax
from jax.sharding import PartitionSpec as P

HEAD_DIM = 128
ROPE_BASE = 500000.0
NORM_EPS = 1e-5


def rms_norm(hidden, norm_gain):
    values = hidden.astype(jnp.float32)
    inv_rms = lax.rsqrt(jnp.mean(values * values, axis=-1, keepdims=True) + NORM_EPS)
    return (values * inv_rms * norm_gain.astype(jnp.float32)).astype(jnp.bfloat16)


def rotary(projected, positions):
    half_dim = HEAD_DIM // 2
    inv_freq = 1.0 / (ROPE_BASE ** (jnp.arange(half_dim, dtype=jnp.float32) * (2.0 / HEAD_DIM)))
    angles = positions.astype(jnp.float32)[:, None] * inv_freq[None, :]
    expand = (angles.shape[0],) + (1,) * (projected.ndim - 2) + (half_dim,)
    cos_table = jnp.cos(angles).reshape(expand)
    sin_table = jnp.sin(angles).reshape(expand)
    first_half = projected[..., :half_dim]
    second_half = projected[..., half_dim:]
    rotated = jnp.concatenate([first_half * cos_table - second_half * sin_table, second_half * cos_table + first_half * sin_table], axis=-1)
    return rotated.astype(jnp.bfloat16)


def attend_rows(block_queries, block_pos, cache_keys, cache_values, cache_valid, new_keys, new_values, all_pos):
    score_scale = 1.0 / math.sqrt(HEAD_DIM)
    cache_scores = jnp.einsum('rkgd,skd->krgs', block_queries, cache_keys, preferred_element_type=jnp.float32) * score_scale
    new_scores = jnp.einsum('rkgd,skd->krgs', block_queries, new_keys, preferred_element_type=jnp.float32) * score_scale
    cache_scores = jnp.where(cache_valid, cache_scores, -jnp.inf)
    causal = all_pos[None, None, None, :] <= block_pos[None, :, None, None]
    new_scores = jnp.where(causal, new_scores, -jnp.inf)
    row_max = jnp.maximum(jnp.max(cache_scores, axis=-1, keepdims=True), jnp.max(new_scores, axis=-1, keepdims=True))
    cache_probs = jnp.exp(cache_scores - row_max)
    new_probs = jnp.exp(new_scores - row_max)
    normalizer = jnp.sum(cache_probs, axis=-1, keepdims=True) + jnp.sum(new_probs, axis=-1, keepdims=True)
    weighted = jnp.einsum('krgs,skd->krgd', cache_probs.astype(jnp.bfloat16), cache_values, preferred_element_type=jnp.float32)
    weighted = weighted + jnp.einsum('krgs,skd->krgd', new_probs.astype(jnp.bfloat16), new_values, preferred_element_type=jnp.float32)
    return jnp.transpose((weighted / normalizer).astype(jnp.bfloat16), (1, 0, 2, 3))


def solution(mesh):
    tp_size = mesh.shape['tp']
    token_spec = P(('dp', 'cp', 'tp'), None)
    column_spec = P(None, 'tp')
    row_spec = P('tp', None)

    def device_layer(hidden_loc, pos_loc, cache_len, cache_k, cache_v, norm1_gain, w_query, w_key, w_value, w_out, norm2_gain, w_gate, w_up, w_down):
        shard_rows = hidden_loc.shape[0]
        kv_local = w_key.shape[1] // HEAD_DIM
        groups = w_query.shape[1] // w_key.shape[1]
        normed = rms_norm(hidden_loc, norm1_gain)
        group_in = lax.all_gather(normed, 'tp', axis=0, tiled=True)
        group_pos = lax.all_gather(pos_loc, 'tp', axis=0, tiled=True)
        group_rows = group_in.shape[0]
        queries = rotary(jnp.dot(group_in, w_query, preferred_element_type=jnp.float32).reshape(group_rows, kv_local, groups, HEAD_DIM), group_pos)
        keys_loc = rotary(jnp.dot(group_in, w_key, preferred_element_type=jnp.float32).reshape(group_rows, kv_local, HEAD_DIM), group_pos)
        values_loc = jnp.dot(group_in, w_value, preferred_element_type=jnp.float32).astype(jnp.bfloat16).reshape(group_rows, kv_local, HEAD_DIM)
        new_keys = lax.all_gather(keys_loc, 'cp', axis=0, tiled=True)
        new_values = lax.all_gather(values_loc, 'cp', axis=0, tiled=True)
        all_pos = lax.all_gather(group_pos, 'cp', axis=0, tiled=True)
        cache_keys = lax.all_gather(lax.all_to_all(cache_k, 'tp', 1, 0, tiled=True), 'cp', axis=0, tiled=True).reshape(-1, kv_local, HEAD_DIM)
        cache_values = lax.all_gather(lax.all_to_all(cache_v, 'tp', 1, 0, tiled=True), 'cp', axis=0, tiled=True).reshape(-1, kv_local, HEAD_DIM)
        cache_valid = jnp.arange(cache_keys.shape[0]) < cache_len[0]
        block_queries = queries.reshape(tp_size, shard_rows, kv_local, groups, HEAD_DIM)
        block_pos = group_pos.reshape(tp_size, shard_rows)

        def attend_block(block_item):
            return attend_rows(block_item[0], block_item[1], cache_keys, cache_values, cache_valid, new_keys, new_values, all_pos)

        attended = lax.map(attend_block, (block_queries, block_pos)).reshape(group_rows, kv_local * groups * HEAD_DIM)
        attn_part = jnp.dot(attended, w_out, preferred_element_type=jnp.float32)
        residual_mid = (hidden_loc.astype(jnp.float32) + lax.psum_scatter(attn_part, 'tp', scatter_dimension=0, tiled=True)).astype(jnp.bfloat16)
        group_mid = lax.all_gather(rms_norm(residual_mid, norm2_gain), 'tp', axis=0, tiled=True)
        gate_proj = jnp.dot(group_mid, w_gate, preferred_element_type=jnp.float32)
        up_proj = jnp.dot(group_mid, w_up, preferred_element_type=jnp.float32)
        hidden_mlp = (jax.nn.silu(gate_proj) * up_proj).astype(jnp.bfloat16)
        mlp_part = jnp.dot(hidden_mlp, w_down, preferred_element_type=jnp.float32)
        return (residual_mid.astype(jnp.float32) + lax.psum_scatter(mlp_part, 'tp', scatter_dimension=0, tiled=True)).astype(jnp.bfloat16)

    return jax.shard_map(device_layer, mesh=mesh, in_specs=(token_spec, P(('dp', 'cp', 'tp')), P('dp'), token_spec, token_spec, P(), column_spec, column_spec, column_spec, row_spec, P(), column_spec, column_spec, row_spec), out_specs=token_spec, check_vma=False)
```

profile of v0, /device:TPU:1, one launch (start us, length us, event | category | flops | bytes accessed | tf_op | source)
XLA Modules:
  0.0 530.8 jit_solution(8795332723806477726)
XLA Ops:
  6.6 1.4 dynamic-slice
  8.6 0.9 dynamic-update-slice
  9.5 2.8 all-reduce
  12.3 0.7 convert_element_type.68
  13.0 1.1 fusion.50
  14.1 1.1 fusion.52
  15.1 2.1 all_gather.24
  17.2 1.3 convolution_bitcast_fusion
  18.5 0.2 fusion.66
  18.7 0.6 pad_maximum_fusion.1
  19.4 0.0 all-gather.9.cloned.1.call-update
  19.4 0.0 all-gather.13.cloned.1.call-start
  19.4 1.9 convolution_convert_fusion
  21.3 0.0 all-gather.13.cloned.1.call-update
  21.3 0.0 all-gather.11.cloned.1.call-start
  21.4 0.9 copy_bitcast_fusion
  22.3 4.4 all_to_all.38
  26.7 0.0 all-gather.7.cloned.1.call-start
  26.8 0.9 copy_bitcast_fusion.1
  27.7 4.4 all_to_all.39
  32.1 0.0 all-gather.7.cloned.1.call-update
  32.1 0.0 reduce-scatter.3.cloned.1.call-start
  32.2 0.1 reshape.359
  32.2 0.2 multiply_cosine_fusion.1
  32.4 2.7 fusion.73
  35.1 0.1 subtract_convert_fusion
  35.2 0.1 concatenate.29
  35.3 0.1 concatenate.30
  35.5 0.6 pad_maximum_fusion
  36.1 0.4 copy.27
  36.5 150.4 %all-gather.1 = s32[64,1,128]{2,1,0:T(1,128)S(1)} all-gather(s32[1,1,128]{2,1,0:T(1,128)S(1)} %bitcast.125), channel_id=1, replica_groups=mesh['dp'=1,'tp'=2,'cp'=64] {'cp'}, dimensions={0}, use_global_device_ids=true | all-gather | bytes 33280 | tf_op jit(solution)/shard_map/all_gather | solution.py:66
  186.8 4.1 copy.28
  190.9 42.8 %all-gather.11.cloned.1.call-done = bf16[32768,128]{1,0:T(8,128)(2,1)} async-done(((bf16[512,128]{1,0:T(8,128)(2,1)}), bf16[32768,128]{1,0:T(8,128)(2,1)}) %all-gather.11.cloned.1.call-update) | async-done | bytes 8388624 | tf_op jit(solution)/shard_map/all_gather | solution.py:68
  233.7 80.4 %all-gather.7.cloned.1.call-done = bf16[32768,128]{1,0:T(8,128)(2,1)} async-done(((bf16[512,128]{1,0:T(8,128)(2,1)}), bf16[32768,128]{1,0:T(8,128)(2,1)}) %all-gather.7.cloned.1.call-update) | async-done | bytes 8388624 | tf_op jit(solution)/shard_map/all_gather | solution.py:67
  314.0 156.8 %while.11 = (s32[]{:T(128)}, bf16[2,64,1,6,128]{4,1,3,2,0:T(8,128)(2,1)S(1)}, bf16[2,64,1,6,128]{4,1,3,2,0:T(8,128)(2,1)S(1)}, bf16[32768,1,128]{2,0,1:T(8,128)(...) while((s32[]{:T(128)}, ...), condition=%wide.region_6.7_spmd.clone, body=%wide.region_1.6_spmd.clone.sunk | while | flops 8163867648 | bytes 282882560 | solution.py:76
  314.1 0.3 broadcast_compare_fusion.2
  314.4 8.4 %fusion.105 = (f32[64,6]{0,1:T(8,128)S(1)}, f32[64,6,8192]{2,0,1:T(8,128)}) fusion(bf16[8192,1,128]{2,0,1:T(8,128)(2,1)} %get-tuple-element.240, bf16[2,64,1,6,128]{4,1,3,2,0:T(8,128)(2,1)S(1)} %get-tuple-element.236, s32[]{:T(128)} %get-tuple-element.223, pred[64,8192]{1,0:T(8,128)(4,1)S(1)} %broadcast_compare_fusion.2), kind=kOutput, calls=%fused_computation.77.clone.1 | convolution fusion | flops 814743168 | bytes 15304196 | tf_op jit(solution)/shard_map/while/body/eval_jaxpr/rkgd,skd->krgs/dot_general | solution.py:34
  322.9 0.7 iota_compare_fusion.2
  323.6 18.1 %fusion.106 = (f32[64,6]{0,1:T(8,128)S(1)}, f32[64,6,32768]{2,0,1:T(8,128)}) fusion(bf16[32768,1,128]{2,0,1:T(8,128)(2,1)S(1)} %bitcast.118, bf16[2,64,1,6,128]{4,1,3,2,0:T(8,128)(2,1)S(1)} %get-tuple-element.236, s32[]{:T(128)} %get-tuple-element.223, pred[32768]{0:T(1024)(128)(4,1)S(1)} %iota_compare_fusion.2), kind=kOutput, calls=%fused_computation.76.clone.1 | convolution fusion | flops 3258973696 | bytes 58852868 | tf_op jit(solution)/shard_map/while/body/eval_jaxpr/rkgd,skd->krgs/dot_general | solution.py:33
  341.7 6.5 %fusion.109 = f32[64,6]{0,1:T(8,128)S(1)} fusion(f32[64,6,8192]{2,0,1:T(8,128)} %get-tuple-element.208, f32[64,6]{0,1:T(8,128)S(1)} %max.10), kind=kLoop, calls=%fused_computation.9.clone.1 | loop fusion | flops 6291072 | bytes 12585984 | tf_op jit(solution)/shard_map/while/body/eval_jaxpr/reduce_sum | solution.py:41
  348.2 21.5 %fusion.108 = f32[64,6]{0,1:T(8,128)S(1)} fusion(f32[64,6,32768]{2,0,1:T(8,128)} %get-tuple-element.211, f32[64,6]{0,1:T(8,128)S(1)} %max.10), kind=kLoop, calls=%fused_computation.3.clone.1 | loop fusion | flops 25165440 | bytes 50334720 | tf_op jit(solution)/shard_map/while/body/eval_jaxpr/reduce_sum | solution.py:41
  369.8 1.9 fusion.107
  371.7 20.7 %fusion.110 = bf16[2,64,1,6,128]{4,1,3,2,0:T(8,128)(2,1)S(1)} fusion(bf16[2,64,1,6,128]{4,1,3,2,0:T(8,128)(2,1)S(1)} %get-tuple-element.224, s32[]{:T(128)} %get-tuple-element.223, f32[64,6,128]{2,0,1:T(8,128)S(1)} %fusion.107, bf16[32768,1,128]{2,0,1:T(8,128)(2,1)} %get-tuple-element.241, f32[64,6,32768]{2,0,1:T(8,128)} %get-tuple-element.211, ...), kind=kOutput, calls=%fused_computation.21.clone.1 | convolution fusion | flops 3246538752 | bytes 59023364 | tf_op jit(solution)/shard_map/while/body/eval_jaxpr/krgs,skd->krgd/dot_general | solution.py:42
  392.4 0.3 broadcast_compare_fusion.2
  392.7 8.4 %fusion.105 = (f32[64,6]{0,1:T(8,128)S(1)}, f32[64,6,8192]{2,0,1:T(8,128)}) fusion(bf16[8192,1,128]{2,0,1:T(8,128)(2,1)} %get-tuple-element.240, bf16[2,64,1,6,128]{4,1,3,2,0:T(8,128)(2,1)S(1)} %get-tuple-element.236, s32[]{:T(128)} %get-tuple-element.223, pred[64,8192]{1,0:T(8,128)(4,1)S(1)} %broadcast_compare_fusion.2), kind=kOutput, calls=%fused_computation.77.clone.1 | convolution fusion | flops 814743168 | bytes 15304196 | tf_op jit(solution)/shard_map/while/body/eval_jaxpr/rkgd,skd->krgs/dot_general | solution.py:34
  401.1 0.7 iota_compare_fusion.2
  401.8 18.1 %fusion.106 = (f32[64,6]{0,1:T(8,128)S(1)}, f32[64,6,32768]{2,0,1:T(8,128)}) fusion(bf16[32768,1,128]{2,0,1:T(8,128)(2,1)S(1)} %bitcast.118, bf16[2,64,1,6,128]{4,1,3,2,0:T(8,128)(2,1)S(1)} %get-tuple-element.236, s32[]{:T(128)} %get-tuple-element.223, pred[32768]{0:T(1024)(128)(4,1)S(1)} %iota_compare_fusion.2), kind=kOutput, calls=%fused_computation.76.clone.1 | convolution fusion | flops 3258973696 | bytes 58852868 | tf_op jit(solution)/shard_map/while/body/eval_jaxpr/rkgd,skd->krgs/dot_general | solution.py:33
  420.0 6.5 %fusion.109 = f32[64,6]{0,1:T(8,128)S(1)} fusion(f32[64,6,8192]{2,0,1:T(8,128)} %get-tuple-element.208, f32[64,6]{0,1:T(8,128)S(1)} %max.10), kind=kLoop, calls=%fused_computation.9.clone.1 | loop fusion | flops 6291072 | bytes 12585984 | tf_op jit(solution)/shard_map/while/body/eval_jaxpr/reduce_sum | solution.py:41
  426.5 21.5 %fusion.108 = f32[64,6]{0,1:T(8,128)S(1)} fusion(f32[64,6,32768]{2,0,1:T(8,128)} %get-tuple-element.211, f32[64,6]{0,1:T(8,128)S(1)} %max.10), kind=kLoop, calls=%fused_computation.3.clone.1 | loop fusion | flops 25165440 | bytes 50334720 | tf_op jit(solution)/shard_map/while/body/eval_jaxpr/reduce_sum | solution.py:41
  448.0 1.9 fusion.107
  449.9 20.7 %fusion.110 = bf16[2,64,1,6,128]{4,1,3,2,0:T(8,128)(2,1)S(1)} fusion(bf16[2,64,1,6,128]{4,1,3,2,0:T(8,128)(2,1)S(1)} %get-tuple-element.224, s32[]{:T(128)} %get-tuple-element.223, f32[64,6,128]{2,0,1:T(8,128)S(1)} %fusion.107, bf16[32768,1,128]{2,0,1:T(8,128)(2,1)} %get-tuple-element.241, f32[64,6,32768]{2,0,1:T(8,128)} %get-tuple-element.211, ...), kind=kOutput, calls=%fused_computation.21.clone.1 | convolution fusion | flops 3246538752 | bytes 59023364 | tf_op jit(solution)/shard_map/while/body/eval_jaxpr/krgs,skd->krgd/dot_general | solution.py:42
  470.8 0.1 copy.29
  471.0 1.4 fusion.58
  472.3 0.0 reduce-scatter.3.cloned.1.call-update
  472.4 0.0 reduce-scatter.5.cloned.1.call-start
  472.4 11.2 %reduce-scatter.3.cloned.1.call-done = f32[64,1536]{1,0:T(8,128)} async-done(((f32[128,1536]{1,0:T(8,128)}), f32[64,1536]{1,0:T(8,128)}) %reduce-scatter.3.cloned.1.call-update) | async-done | bytes 393232 | tf_op jit(solution)/shard_map/reduce_scatter | solution.py:78
  483.6 1.2 fusion.54
  484.8 0.1 fusion.56
  484.9 2.1 all_gather.31
  487.0 8.3 %fusion.74 = f32[128,4480]{1,0:T(8,128)} fusion(bf16[128,1536]{1,0:T(8,128)(2,1)S(1)} %all_gather.31, bf16[1536,4480]{1,0:T(8,128)(2,1)} %param.27), kind=kOutput, calls=%fused_computation.79 | convolution fusion | flops 1761607680 | bytes 16449536 | tf_op jit(solution)/shard_map/dot_general | solution.py:80
  495.3 14.6 %fusion.49 = f32[128,1536]{1,0:T(8,128)} fusion(bf16[4480,1536]{1,0:T(8,128)(2,1)} %param.29, bf16[128,1536]{1,0:T(8,128)(2,1)S(1)} %all_gather.31, bf16[1536,4480]{1,0:T(8,128)(2,1)} %param.28, f32[128,4480]{1,0:T(8,128)} %fusion.74), kind=kOutput, calls=%fused_computation.36 | convolution fusion | flops 3526656000 | bytes 30998528 | tf_op jit(solution)/shard_map/dot_general | solution.py:83
  509.9 0.0 reduce-scatter.5.cloned.1.call-update
  510.0 12.3 %reduce-scatter.5.cloned.1.call-done = f32[64,1536]{1,0:T(8,128)} async-done(((f32[128,1536]{1,0:T(8,128)}), f32[64,1536]{1,0:T(8,128)}) %reduce-scatter.5.cloned.1.call-update) | async-done | bytes 393232 | tf_op jit(solution)/shard_map/reduce_scatter | solution.py:84
  522.3 1.7 fusion.57
  (51 shorter events, 0.1 us)
Async XLA Ops:
  6.5 464.4 %copy-start = (bf16[768,1536]{1,0:T(8,128)(2,1)S(1)}, bf16[768,1536]{1,0:T(8,128)(2,1)}, u32[]{:S(2)}) copy-start(bf16[768,1536]{1,0:T(8,128)(2,1)} %param.25) | copy-start | bytes 7077892
  6.5 180.3 %all-gather.9.cloned.1.call-start = ((), (), s32[]{:S(2)}) async-start(), calls=%async_computation.5 | async-start | bytes 2129920 | tf_op jit(solution)/shard_map/all_gather | solution.py:64
  19.4 171.6 %all-gather.13.cloned.1.call-start = ((), (), s32[]{:S(2)}) async-start(), calls=%async_computation.9 | async-start | bytes 2129920 | tf_op jit(solution)/shard_map/all_gather | solution.py:65
  21.3 212.4 %all-gather.11.cloned.1.call-start = ((), (), s32[]{:S(2)}) async-start(), calls=%async_computation.6 | async-start | bytes 8519680 | tf_op jit(solution)/shard_map/all_gather | solution.py:68
  26.7 287.3 %all-gather.7.cloned.1.call-start = ((), (), s32[]{:S(2)}) async-start(), calls=%async_computation.4 | async-start | bytes 8519680 | tf_op jit(solution)/shard_map/all_gather | solution.py:67
  32.1 451.5 %reduce-scatter.3.cloned.1.call-start = ((), (), s32[]{:S(2)}) async-start(), calls=%async_computation.7 | async-start | bytes 1179648 | tf_op jit(solution)/shard_map/reduce_scatter | solution.py:78
  314.0 158.4 %copy-start.3 = (bf16[1536]{0:T(1024)(128)(2,1)S(1)}, bf16[1536]{0:T(1024)(128)(2,1)}, u32[]{:S(2)}) copy-start(bf16[1536]{0:T(1024)(128)(2,1)} %param.26) | copy-start | bytes 9220
  314.0 169.6 %copy-start.2 = (bf16[64,1536]{1,0:T(8,128)(2,1)S(1)}, bf16[64,1536]{1,0:T(8,128)(2,1)}, u32[]{:S(2)}) copy-start(bf16[64,1536]{1,0:T(8,128)(2,1)} %param.16) | copy-start | bytes 589828
  314.0 9.5 %slice-start.3 = ((s8[8388608]{0:T(1024)(128)(4,1)}), s8[4194304]{0:T(1024)(128)(4,1)S(1)}, s32[]{:S(2)}) async-start(s8[8388608]{0:T(1024)(128)(4,1)} %bitcast.117), calls=%async_computation.13 | async-start | bytes 8388608 | tf_op jit(solution)/shard_map/while
  314.4 9.1 %slice-start.4 = ((s8[8388608]{0:T(1024)(128)(4,1)}), s8[4194304]{0:T(1024)(128)(4,1)S(1)}, s32[]{:S(2)}) async-start(s8[8388608]{0:T(1024)(128)(4,1)} %bitcast.117), calls=%async_computation.14 | async-start | bytes 8388608 | tf_op jit(solution)/shard_map/while
  341.7 28.0 %slice-start = ((s8[12582912]{0:T(1024)(128)(4,1)}), s8[4194304]{0:T(1024)(128)(4,1)S(1)}, s32[]{:S(2)}) async-start(s8[12582912]{0:T(1024)(128)(4,1)} %bitcast.113), calls=%async_computation.10 | async-start | bytes 8388608 | tf_op jit(solution)/shard_map/while
  348.2 21.5 %slice-start.1 = ((s8[12582912]{0:T(1024)(128)(4,1)}), s8[4194304]{0:T(1024)(128)(4,1)S(1)}, s32[]{:S(2)}) async-start(s8[12582912]{0:T(1024)(128)(4,1)} %bitcast.113), calls=%async_computation.11 | async-start | bytes 8388608 | tf_op jit(solution)/shard_map/while
  348.2 21.5 %slice-start.2 = ((s8[12582912]{0:T(1024)(128)(4,1)}), s8[4194304]{0:T(1024)(128)(4,1)S(1)}, s32[]{:S(2)}) async-start(s8[12582912]{0:T(1024)(128)(4,1)} %bitcast.113), calls=%async_computation.12 | async-start | bytes 8388608 | tf_op jit(solution)/shard_map/while
  348.2 21.5 %copy-start.1 = (bf16[8192,1,128]{2,0,1:T(8,128)(2,1)S(1)}, bf16[8192,1,128]{2,0,1:T(8,128)(2,1)}, u32[]{:S(2)}) copy-start(bf16[8192,1,128]{2,0,1:T(8,128)(2,1)} %get-tuple-element.242) | copy-start | bytes 6291460 | tf_op jit(solution)/shard_map/while
  392.3 9.5 %slice-start.3 = ((s8[8388608]{0:T(1024)(128)(4,1)}), s8[4194304]{0:T(1024)(128)(4,1)S(1)}, s32[]{:S(2)}) async-start(s8[8388608]{0:T(1024)(128)(4,1)} %bitcast.117), calls=%async_computation.13 | async-start | bytes 8388608 | tf_op jit(solution)/shard_map/while
  392.7 9.1 %slice-start.4 = ((s8[8388608]{0:T(1024)(128)(4,1)}), s8[4194304]{0:T(1024)(128)(4,1)S(1)}, s32[]{:S(2)}) async-start(s8[8388608]{0:T(1024)(128)(4,1)} %bitcast.117), calls=%async_computation.14 | async-start | bytes 8388608 | tf_op jit(solution)/shard_map/while
  420.0 28.0 %slice-start = ((s8[12582912]{0:T(1024)(128)(4,1)}), s8[4194304]{0:T(1024)(128)(4,1)S(1)}, s32[]{:S(2)}) async-start(s8[12582912]{0:T(1024)(128)(4,1)} %bitcast.113), calls=%async_computation.10 | async-start | bytes 8388608 | tf_op jit(solution)/shard_map/while
  426.5 21.5 %slice-start.1 = ((s8[12582912]{0:T(1024)(128)(4,1)}), s8[4194304]{0:T(1024)(128)(4,1)S(1)}, s32[]{:S(2)}) async-start(s8[12582912]{0:T(1024)(128)(4,1)} %bitcast.113), calls=%async_computation.11 | async-start | bytes 8388608 | tf_op jit(solution)/shard_map/while
  426.5 21.5 %slice-start.2 = ((s8[12582912]{0:T(1024)(128)(4,1)}), s8[4194304]{0:T(1024)(128)(4,1)S(1)}, s32[]{:S(2)}) async-start(s8[12582912]{0:T(1024)(128)(4,1)} %bitcast.113), calls=%async_computation.12 | async-start | bytes 8388608 | tf_op jit(solution)/shard_map/while
  426.5 21.5 %copy-start.1 = (bf16[8192,1,128]{2,0,1:T(8,128)(2,1)S(1)}, bf16[8192,1,128]{2,0,1:T(8,128)(2,1)}, u32[]{:S(2)}) copy-start(bf16[8192,1,128]{2,0,1:T(8,128)(2,1)} %get-tuple-element.242) | copy-start | bytes 6291460 | tf_op jit(solution)/shard_map/while
  472.4 49.9 %reduce-scatter.5.cloned.1.call-start = ((), (), s32[]{:S(2)}) async-start(), calls=%async_computation.8 | async-start | bytes 1179648 | tf_op jit(solution)/shard_map/reduce_scatter | solution.py:84
Sparse Core Ops, SparseCore 0:
  19.5 67.0 all-gather.8
  89.5 63.6 all-gather.12
  156.1 77.5 all-gather.10
  236.4 77.5 all-gather.6
  472.5 11.0 reduce-scatter.2
  510.1 12.1 reduce-scatter.4
where the time goes:
time: 532 us; the launch traced here: 531 us
  blocking collectives  166 us (31%)
  waiting for transfers between devices  147 us (28%)
  matrix products  128 us (24%)
  other arithmetic  65.6 us (12%)
  between operations  14.3 us (3%)
  local copies, waits for them, and re-layouts  9.11 us (2%)
    all_gather x1, blocking collectives, device_layer(): all_pos = lax.all_gather(group_pos, 'cp', axis=0, tiled=True)  150 us
    all_gather x1, waiting for transfers between devices, device_layer(): lax.all_gather(lax.all_to_all(cache_k, 'tp', 1, 0, tiled=True), 'cp', axi...  80.4 us
    reduce_sum x2, other arithmetic, attend_rows(): jnp.sum(cache_probs, axis=-1, keepdims=True)  43 us
    all_gather x1, waiting for transfers between devices, device_layer(): lax.all_gather(lax.all_to_all(cache_v, 'tp', 1, 0, tiled=True), 'cp', axi...  42.8 us
    dot_general x2, matrix products, attend_rows(): jnp.einsum('krgs,skd->krgd', cache_probs.astype(jnp.bfloat16), cache_valu...  41.3 us
    dot_general x2, matrix products, attend_rows(): jnp.einsum('rkgd,skd->krgs', block_queries, cache_keys, preferred_element...  36.3 us
    dot_general x2, matrix products, attend_rows(): jnp.einsum('rkgd,skd->krgs', block_queries, new_keys, preferred_element_t...  16.9 us
    dot_general x1, matrix products, device_layer(): mlp_part = jnp.dot(hidden_mlp, w_down, preferred_element_type=jnp.float32)  14.6 us
  transfers between devices with their start and end apart: 6, of which 4 were waited for; matrix products, arithmetic and copies ran while one was open for 2% of the time, Pallas kernels for 0%

commit v1 on v0

v1 whole, which is shorter than its diff:
```python
import functools
import math
import jax
import jax.numpy as jnp
from jax import lax
from jax.experimental import pallas as pl
from jax.experimental.pallas import tpu as pltpu
from jax.sharding import PartitionSpec as P

HEAD_DIM = 128
ROPE_BASE = 500000.0
NORM_EPS = 1e-5
HEADS = 6
SLOTS = 256
COLS = HEADS * 64
QW = 4 * COLS
NEG = -2.3e38
EXP_C = math.log2(math.e) / math.sqrt(HEAD_DIM)
BUCKETS = (16,)


def rms_norm(hidden, norm_gain):
    values = hidden.astype(jnp.float32)
    inv_rms = lax.rsqrt(jnp.mean(values * values, axis=-1, keepdims=True) + NORM_EPS)
    return (values * inv_rms * norm_gain.astype(jnp.float32)).astype(jnp.bfloat16)


def rotary(projected, positions):
    half_dim = HEAD_DIM // 2
    inv_freq = 1.0 / (ROPE_BASE ** (jnp.arange(half_dim, dtype=jnp.float32) * (2.0 / HEAD_DIM)))
    angles = positions.astype(jnp.float32)[:, None] * inv_freq[None, :]
    expand = (angles.shape[0],) + (1,) * (projected.ndim - 2) + (half_dim,)
    cos_table = jnp.cos(angles).reshape(expand)
    sin_table = jnp.sin(angles).reshape(expand)
    first_half = projected[..., :half_dim]
    second_half = projected[..., half_dim:]
    rotated = jnp.concatenate([first_half * cos_table - second_half * sin_table, second_half * cos_table + first_half * sin_table], axis=-1)
    return rotated.astype(jnp.bfloat16)


def plane_of(cyc, k):
    major = k // 4
    minor = (k - major) % 4
    return (4 * major + minor) * (1 - cyc) + (4 * minor + major) * cyc


def attend_kernel(nb, mask_from, len_ref, qt_ref, kvn_ref, ck_ref, cv_ref, out_ref,
                  QT, KC, VC, KVN, ACC, PART, VTS,
                  send_sem, recv_sem, q_send, q_recv, o_send, o_recv, sib_send, sib_recv, loc_sem):
    c = lax.axis_index('cp')
    t = lax.axis_index('tp')
    z, y, x = c // 16, (c // 4) % 4, c % 4
    g = 4 * z + y
    k_own = (4 * z + (y + z) % 4, 4 * y + (y + z) % 4)
    cache_len = len_ref[0]

    def dev(core, chip):
        return {'tp': core, 'cp': chip}

    def ring_k(cyc):
        return k_own[0] * (1 - cyc) + k_own[1] * cyc

    def neighbour(cyc, d):
        return plane_of(cyc, (ring_k(cyc) + 1 + 14 * d) % 16) * 4 + x

    def block_of(cyc, d, j):
        return plane_of(cyc, (ring_k(cyc) + 16 + (2 * d - 1) * j) % 16)

    barrier = pltpu.get_barrier_semaphore()
    partners = [dev(t, neighbour(cyc, d)) for cyc in (0, 1) for d in (0, 1)]
    partners += [dev(t, g * 4 + (x + dx) % 4) for dx in (1, 2, 3)] + [dev(1 - t, c)]
    VTS[...] = cv_ref[...].T
    for p in partners:
        pl.semaphore_signal(barrier, inc=1, device_id=p, device_id_type=pl.DeviceIdType.MESH)
    pl.semaphore_wait(barrier, len(partners))

    def q_copy(dx):
        return pltpu.make_async_remote_copy(
            src_ref=qt_ref, dst_ref=QT.at[:, :, pl.ds(pl.multiple_of(x * COLS, 128), COLS)],
            send_sem=q_send.at[dx - 1], recv_sem=q_recv.at[dx - 1],
            device_id=dev(t, g * 4 + (x + dx) % 4), device_id_type=pl.DeviceIdType.MESH)

    def q_land(dx):
        src_x = (x + 4 - dx) % 4
        return pltpu.make_async_remote_copy(
            src_ref=qt_ref, dst_ref=QT.at[:, :, pl.ds(pl.multiple_of(src_x * COLS, 128), COLS)],
            send_sem=q_send.at[dx - 1], recv_sem=q_recv.at[dx - 1],
            device_id=dev(t, g * 4 + (x + dx) % 4), device_id_type=pl.DeviceIdType.MESH)

    mine = pl.ds(pl.multiple_of(t * 128, 128), 128)
    other = pl.ds(pl.multiple_of((1 - t) * 128, 128), 128)

    def sib_copies(half):
        return (pltpu.make_async_remote_copy(
                    src_ref=ck_ref.at[:, other], dst_ref=KC.at[half, g], send_sem=sib_send.at[0], recv_sem=sib_recv.at[0],
                    device_id=dev(1 - t, c), device_id_type=pl.DeviceIdType.MESH),
                pltpu.make_async_remote_copy(
                    src_ref=VTS.at[other], dst_ref=VC.at[half, g], send_sem=sib_send.at[1], recv_sem=sib_recv.at[1],
                    device_id=dev(1 - t, c), device_id_type=pl.DeviceIdType.MESH))

    local = [pltpu.make_async_copy(qt_ref, QT.at[:, :, pl.ds(pl.multiple_of(x * COLS, 128), COLS)], loc_sem.at[0]),
             pltpu.make_async_copy(kvn_ref, KVN.at[g], loc_sem.at[1])]
    local_cache = [pltpu.make_async_copy(ck_ref.at[:, mine], KC.at[t, g], loc_sem.at[2]),
                   pltpu.make_async_copy(VTS.at[mine], VC.at[t, g], loc_sem.at[3])]

    @pl.when(g < nb)
    def _():
        for cp in sib_copies(t):
            cp.start()
        for cp in local_cache:
            cp.start()
    for cp in local:
        cp.start()
    for dx in (2, 1, 3):
        q_copy(dx).start()

    def ring_copy(cyc, d, kind, s, place):
        buf = (KC.at[cyc, place], VC.at[cyc, place], KVN.at[place, cyc])[kind]
        return pltpu.make_async_remote_copy(
            src_ref=buf, dst_ref=buf, send_sem=send_sem.at[cyc, d, kind, s], recv_sem=recv_sem.at[cyc, d, kind, s],
            device_id=dev(t, neighbour(cyc, d)), device_id_type=pl.DeviceIdType.MESH)

    def for_copies(s, fn, back):
        for kind in range(3):
            for cyc in (0, 1):
                for d in (0, 1):
                    place = block_of(cyc, d, s - back)
                    live = s <= 8 - d
                    if kind < 2:
                        live = jnp.logical_and(live, place < nb)

                    @pl.when(live)
                    def _():
                        fn(ring_copy(cyc, d, kind, s, place))

    for cp in local:
        cp.wait()

    @pl.when(g < nb)
    def _():
        for cp in local_cache:
            cp.wait()
        for cp in sib_copies(1 - t):
            cp.wait_recv()

    for_copies(1, lambda cp: cp.start(), 1)

    ACC[:, 128:136, :] = jnp.where(lax.broadcasted_iota(jnp.int32, (2, 8, QW), 1) == 0, NEG, 0.0)
    ACC[:, 0:128, :] = jnp.zeros((2, 128, QW), jnp.float32)

    def units(half, tiles, key, val_t, mask):
        cols = [pl.ds(pl.multiple_of(tile * 256, 256), 256) for tile in tiles]
        scores = [jnp.dot(key, QT[half, :, col], preferred_element_type=jnp.float32) for col in cols]
        if mask is not None:
            scores = [mask(tile, s) for tile, s in zip(tiles, scores)]
        for col, s in zip(cols, scores):
            old_max = ACC[half, 128:129, col]
            new_max = jnp.maximum(old_max, jnp.max(s, axis=0, keepdims=True))
            probs = jnp.exp2(s * EXP_C - new_max * EXP_C)
            alpha = jnp.exp2((old_max - new_max) * EXP_C)
            ACC[half, 128:129, col] = new_max
            ACC[half, 129:130, col] = ACC[half, 129:130, col] * alpha + jnp.sum(probs, axis=0, keepdims=True)
            ACC[half, 0:128, col] = ACC[half, 0:128, col] * alpha + jnp.dot(
                val_t, probs.astype(jnp.bfloat16), preferred_element_type=jnp.float32)

    def cache_block(cyc, place):
        limit = cache_len - (4 * place + x) * (2 * SLOTS) - cyc * SLOTS

        def run(mask):
            def body(i, carry):
                half = i // 3
                pair = i % 3
                units(half, (2 * pair, 2 * pair + 1), KC[cyc, place], VC[cyc, place], mask)
                return carry
            lax.fori_loop(0, 6, body, 0)

        def slot_mask(tile, s):
            return jnp.where(lax.broadcasted_iota(jnp.int32, s.shape, 0) < limit, s, NEG)

        if mask_from > 0:
            @pl.when(place < mask_from)
            def _():
                run(None)

        @pl.when(place >= mask_from)
        def _():
            run(slot_mask)

    for dx in (1, 3, 2):
        q_land(dx).wait_recv()

    def step(s, carry):
        for_copies(s, lambda cp: cp.wait_recv(), 0)
        for_copies(s + 1, lambda cp: cp.start(), 1)
        j = s - 1

        def block(b, inner):
            cyc, d = b // 2, b % 2
            place = block_of(cyc, d, j)
            live = jnp.logical_and(place < nb, jnp.logical_or(d == 0, jnp.logical_and(j > 0, j < 8)))

            @pl.when(live)
            def _():
                cache_block(cyc, place)
            return inner
        lax.fori_loop(0, 4, block, 0)
        return carry

    lax.fori_loop(1, 10, step, 0)

    edge = g // 4

    def new_item(n, carry):
        j = n - 4
        masked_hi = jnp.logical_and(n >= 4, j > edge).astype(jnp.int32)
        masked_lo = jnp.logical_and(n >= 4, j <= edge).astype(jnp.int32)
        full = (n < 4).astype(jnp.int32)
        q_half = 1 - masked_lo
        k_half = masked_hi
        blk = full * n + masked_lo * j + masked_hi * (j - 1)
        places = pl.ds(blk * 4, 4)
        key = KVN[places, :, 0, k_half].reshape(256, 128)
        val_t = KVN[places, :, 1, k_half].reshape(256, 128).T

        def causal(tile, s):
            row = lax.broadcasted_iota(jnp.int32, (256, 1), 0)
            run = 2 * (4 * (blk * 4 + row // 64) + x) + (row % 64) // 32
            key_pos = (run + k_half * (255 - 2 * run)) * 32 + row % 32
            col = lax.broadcasted_iota(jnp.int32, (1, 256), 1) + tile * 256
            q_run = 2 * (4 * g + col // COLS) + (col % 64) // 32
            q_pos = (q_run + q_half * (255 - 2 * q_run)) * 32 + col % 32
            return jnp.where(key_pos <= q_pos, s, NEG)

        def body(i, inner):
            units(q_half, (2 * i, 2 * i + 1), key, val_t, causal)
            return inner
        lax.fori_loop(0, 3, body, 0)
        return carry

    lax.fori_loop(0, 9, new_item, 0)

    def o_copy(dx):
        dst_x = (x + dx) % 4
        return pltpu.make_async_remote_copy(
            src_ref=ACC.at[:, :, pl.ds(pl.multiple_of(dst_x * COLS, 128), COLS)], dst_ref=PART.at[dx - 1],
            send_sem=o_send.at[dx - 1], recv_sem=o_recv.at[dx - 1],
            device_id=dev(t, g * 4 + dst_x), device_id_type=pl.DeviceIdType.MESH)

    for dx in (2, 1, 3):
        o_copy(dx).start()
    for dx in (1, 3, 2):
        o_copy(dx).wait_recv()
    own = pl.ds(pl.multiple_of(x * COLS, 128), COLS)
    for half in (0, 1):
        maxes = [ACC[half, 128:129, own]] + [PART[i, half, 128:129, :] for i in range(3)]
        sums = [ACC[half, 129:130, own]] + [PART[i, half, 129:130, :] for i in range(3)]
        top = functools.reduce(jnp.maximum, maxes)
        weights = [jnp.exp2((m - top) * EXP_C) for m in maxes]
        total = sum(w * l for w, l in zip(weights, sums))
        acc = ACC[half, 0:128, own] * weights[0]
        for i in range(3):
            acc = acc + PART[i, half, 0:128, :] * weights[i + 1]
        o_rows = (acc / total).T.astype(jnp.bfloat16)
        for head in range(HEADS):
            for core in (0, 1):
                out_ref[core * 64 + half * 32:core * 64 + half * 32 + 32, head * 128:head * 128 + 128] = \
                    o_rows[head * 64 + core * 32:head * 64 + core * 32 + 32, :]

    for dx in (1, 2, 3):
        q_copy(dx).wait_send()
        o_copy(dx).wait_send()

    @pl.when(g < nb)
    def _():
        for cp in sib_copies(t):
            cp.wait_send()

    def drain(s, carry):
        for_copies(s, lambda cp: cp.wait_send(), 1)
        return carry
    lax.fori_loop(1, 9, drain, 0)


def attend(index, nb, mask_from, cache_len, q_t, kv_new, cache_k, cache_v):
    bf16, f32 = jnp.bfloat16, jnp.float32
    vmem = pl.BlockSpec(memory_space=pltpu.VMEM)
    return pl.pallas_call(
        functools.partial(attend_kernel, nb, mask_from),
        out_shape=jax.ShapeDtypeStruct((128, HEADS * HEAD_DIM), bf16),
        in_specs=[pl.BlockSpec(memory_space=pltpu.SMEM), vmem, vmem, vmem, vmem],
        out_specs=vmem,
        scratch_shapes=[
            pltpu.VMEM((2, 128, QW), bf16),
            pltpu.VMEM((2, 16, SLOTS, 128), bf16),
            pltpu.VMEM((2, 16, 128, SLOTS), bf16),
            pltpu.VMEM((16, 2, 2, 2, 32, 128), bf16),
            pltpu.VMEM((2, 136, QW), f32),
            pltpu.VMEM((3, 2, 136, COLS), f32),
            pltpu.VMEM((256, SLOTS), bf16),
            pltpu.SemaphoreType.DMA((2, 2, 3, 9)),
            pltpu.SemaphoreType.DMA((2, 2, 3, 9)),
            pltpu.SemaphoreType.DMA((3,)),
            pltpu.SemaphoreType.DMA((3,)),
            pltpu.SemaphoreType.DMA((3,)),
            pltpu.SemaphoreType.DMA((3,)),
            pltpu.SemaphoreType.DMA((2,)),
            pltpu.SemaphoreType.DMA((2,)),
            pltpu.SemaphoreType.DMA((4,)),
        ],
        compiler_params=pltpu.CompilerParams(collective_id=index, has_side_effects=True, vmem_limit_bytes=48 * 1024 * 1024),
        name='attend_%d' % nb,
    )(cache_len, q_t, kv_new, cache_k, cache_v)


def solution(mesh):
    token_spec = P(('dp', 'cp', 'tp'), None)
    column_spec = P(None, 'tp')
    row_spec = P('tp', None)

    def device_layer(hidden_loc, pos_loc, cache_len, cache_k, cache_v, norm1_gain, w_query, w_key, w_value, w_out, norm2_gain, w_gate, w_up, w_down):
        normed = rms_norm(hidden_loc, norm1_gain)
        group_in = lax.all_gather(normed, 'tp', axis=0, tiled=True)
        group_pos = lax.all_gather(pos_loc, 'tp', axis=0, tiled=True)
        rows = group_in.shape[0]
        queries = rotary(jnp.dot(group_in, w_query, preferred_element_type=jnp.float32).reshape(rows, HEADS, HEAD_DIM), group_pos)
        keys_new = rotary(jnp.dot(group_in, w_key, preferred_element_type=jnp.float32), group_pos)
        values_new = jnp.dot(group_in, w_value, preferred_element_type=jnp.float32).astype(jnp.bfloat16)
        q_t = jnp.transpose(queries.reshape(2, 2, 32, HEADS, HEAD_DIM), (1, 4, 3, 0, 2)).reshape(2, HEAD_DIM, COLS)
        kv_new = jnp.stack([keys_new.reshape(2, 2, 32, HEAD_DIM), values_new.reshape(2, 2, 32, HEAD_DIM)], axis=1)
        attended = attend(0, 16, 0, cache_len, q_t, kv_new, cache_k, cache_v)
        attn_part = jnp.dot(attended, w_out, preferred_element_type=jnp.float32)
        residual_mid = (hidden_loc.astype(jnp.float32) + lax.psum_scatter(attn_part, 'tp', scatter_dimension=0, tiled=True)).astype(jnp.bfloat16)
        group_mid = lax.all_gather(rms_norm(residual_mid, norm2_gain), 'tp', axis=0, tiled=True)
        gate_proj = jnp.dot(group_mid, w_gate, preferred_element_type=jnp.float32)
        up_proj = jnp.dot(group_mid, w_up, preferred_element_type=jnp.float32)
        hidden_mlp = (jax.nn.silu(gate_proj) * up_proj).astype(jnp.bfloat16)
        mlp_part = jnp.dot(hidden_mlp, w_down, preferred_element_type=jnp.float32)
        return (residual_mid.astype(jnp.float32) + lax.psum_scatter(mlp_part, 'tp', scatter_dimension=0, tiled=True)).astype(jnp.bfloat16)

    return jax.shard_map(device_layer, mesh=mesh, in_specs=(token_spec, P(('dp', 'cp', 'tp')), P('dp'), token_spec, token_spec, P(), column_spec, column_spec, column_spec, row_spec, P(), column_spec, column_spec, row_spec), out_specs=token_spec, check_vma=False)
```

time: 532 us -> 268 us (0.50)
  Pallas kernels: 0 us -> 184 us
  blocking collectives: 166 us -> 7 us
  waiting for transfers between devices: 147 us -> 24.3 us
  matrix products: 128 us -> 27.9 us
  other arithmetic: 65.6 us -> 6.45 us
  local copies, waits for them, and re-layouts: 9.11 us -> 2.91 us
    pallas_call x0 -> x1, Pallas kernels: none -> 184 us  [attend(): pl.pallas_call(functools.partial(attend_kernel, nb, mask_from), out_shape...]
    all_gather x1 -> x0, blocking collectives: 150 us -> none  [device_layer(): all_pos = lax.all_gather(group_pos, 'cp', axis=0, tiled=True)]
    all_gather x4 -> x0, waiting for transfers between devices: 123 us -> none  [the longest x1 80.4 us: device_layer(): lax.all_gather(lax.all_to_all(cache_k, 'tp', 1, 0, tiled=True), 'cp', axi...]
    dot_general x8 -> x0, matrix products: 98.2 us -> none  [the longest x2 41.3 us: attend_rows(): jnp.einsum('krgs,skd->krgd', cache_probs.astype(jnp.bfloat16), cache_valu...]
    reduce_sum x4 -> x0, other arithmetic: 56 us -> none  [the longest x2 43 us: attend_rows(): jnp.sum(cache_probs, axis=-1, keepdims=True)]
    all_to_all x2 -> x0, blocking collectives: 8.77 us -> none  [the longest x1 4.4 us: device_layer(): lax.all_to_all(cache_v, 'tp', 1, 0, tiled=True)]
  transfers between devices with their start and end apart: 6 -> 2, of which waited for: 4 -> 2; matrix products, arithmetic and copies ran while one was open for 2% -> 0% of each run, Pallas kernels for 0% -> 0%
where the time goes in v1:
time: 268 us; the launch traced here: 267 us
  Pallas kernels  184 us (69%)
  matrix products  27.9 us (10%)
  waiting for transfers between devices  24.3 us (9%)
  between operations  15.1 us (6%)
  blocking collectives  7 us (3%)
  other arithmetic  6.45 us (2%)
  local copies, waits for them, and re-layouts  2.91 us (1%)
    pallas_call x1, Pallas kernels, attend(): pl.pallas_call(functools.partial(attend_kernel, nb, mask_from), out_shape...  184 us
    dot_general x1, matrix products, device_layer(): mlp_part = jnp.dot(hidden_mlp, w_down, preferred_element_type=jnp.float32)  14.6 us
    reduce_scatter x1, waiting for transfers between devices, device_layer(): lax.psum_scatter(mlp_part, 'tp', scatter_dimension=0, tiled=True)  12.3 us
    reduce_scatter x1, waiting for transfers between devices, device_layer(): lax.psum_scatter(attn_part, 'tp', scatter_dimension=0, tiled=True)  12 us
    dot_general x1, matrix products, device_layer(): gate_proj = jnp.dot(group_mid, w_gate, preferred_element_type=jnp.float32)  8.32 us
  transfers between devices with their start and end apart: 2, of which 2 were waited for; matrix products, arithmetic and copies ran while one was open for 0% of the time, Pallas kernels for 0%

profile of v1, /device:TPU:1, one launch (start us, length us, event | category | flops | bytes accessed | tf_op | source)
XLA Modules:
  0.0 267.4 jit_solution(10510814216017956506)
XLA Ops:
  6.5 0.0 copy-start
  6.5 0.0 reduce-scatter.3.cloned.1.call-start
  7.4 1.1 fusion.2
  8.4 1.2 dynamic-slice
  10.4 0.9 dynamic-update-slice
  11.2 2.8 %all-reduce = s32[128]{0:T(128)S(1)} all-reduce(s32[128]{0:T(128)S(1)} %dynamic-update-slice), channel_id=1, replica_groups=mesh['dp'=1,'tp'=2,'cp'=64] {'tp'}, use_global_device_ids=true, to_apply=%add | all-reduce | flops 128 | bytes 1024
  14.0 0.0 copy-start.3
  14.0 0.8 convert_element_type.47
  14.9 1.0 fusion.4
  15.9 2.1 all_gather.9
  18.0 1.3 convolution_convert_fusion
  19.3 1.3 fusion.13
  20.6 0.0 copy-done.3
  20.6 0.0 copy-start.1
  20.6 0.0 copy-start.2
  20.6 1.1 fusion.12
  21.7 0.2 subtract_convert_fusion.1
  21.9 0.1 copy.23
  22.0 0.1 copy.24
  22.1 0.1 subtract_convert_fusion
  22.2 0.2 copy.20
  22.4 0.2 copy.21
  22.6 0.1 maximum_bitcast_fusion
  22.7 0.2 copy.25.qt_ref
  22.9 0.1 pad_maximum_fusion.kvn_ref
  23.0 0.0 copy-done.1
  23.0 0.0 copy-done.2
  23.0 0.0 copy-start.5
  23.0 0.0 copy-start.4
  23.1 183.6 %attend_16.1 = bf16[128,768]{1,0:T(8,128)(2,1)S(1)} custom-call(s32[1]{0:T(128)S(6)} %copy.28.len_ref, bf16[2,128,384]{2,1,0:T(8,128)(2,1)S(1)} %copy.25.qt_ref, bf16[2,2,2,32,128]{4,3,2,1,0:T(8,128)(2,1)S(1)} %pad_maximum_fusion.kvn_ref, bf16[256,256]{1,0:T(8,128)(2,1)S(1)} %copy-done.1, bf16[256,256]{1,0:T(8,128)(2,1)S(1)} %copy-done.2), custom_call_target="tpu_custom_call" | custom-call | tf_op jit(solution)/shard_map/attend_16/pallas_call | solution.py:287
  206.7 0.0 copy-done
  206.7 1.4 fusion.14
  208.1 0.0 reduce-scatter.3.cloned.1.call-update
  208.1 0.0 reduce-scatter.5.cloned.1.call-start
  208.1 0.0 copy-done.5
  208.2 12.0 %reduce-scatter.3.cloned.1.call-done = f32[64,1536]{1,0:T(8,128)} async-done(((f32[128,1536]{1,0:T(8,128)}), f32[64,1536]{1,0:T(8,128)}) %reduce-scatter.3.cloned.1.call-update) | async-done | bytes 393232 | tf_op jit(solution)/shard_map/reduce_scatter | solution.py:332
  220.1 0.0 copy-done.4
  220.1 1.2 fusion.6
  221.3 0.1 fusion.8
  221.4 2.1 all_gather.11
  223.5 8.3 %fusion.15 = f32[128,4480]{1,0:T(8,128)} fusion(bf16[128,1536]{1,0:T(8,128)(2,1)S(1)} %all_gather.11, bf16[1536,4480]{1,0:T(8,128)(2,1)} %param.25), kind=kOutput, calls=%fused_computation.33 | convolution fusion | flops 1761607680 | bytes 16449536 | tf_op jit(solution)/shard_map/dot_general | solution.py:334
  231.8 14.6 %fusion.1 = f32[128,1536]{1,0:T(8,128)} fusion(bf16[4480,1536]{1,0:T(8,128)(2,1)} %param.27, bf16[128,1536]{1,0:T(8,128)(2,1)S(1)} %all_gather.11, bf16[1536,4480]{1,0:T(8,128)(2,1)} %param.26, f32[128,4480]{1,0:T(8,128)} %fusion.15), kind=kOutput, calls=%fused_computation.3 | convolution fusion | flops 3526656000 | bytes 30998528 | tf_op jit(solution)/shard_map/dot_general | solution.py:337
  246.4 0.0 reduce-scatter.5.cloned.1.call-update
  246.5 12.3 %reduce-scatter.5.cloned.1.call-done = f32[64,1536]{1,0:T(8,128)} async-done(((f32[128,1536]{1,0:T(8,128)}), f32[64,1536]{1,0:T(8,128)}) %reduce-scatter.5.cloned.1.call-update) | async-done | bytes 393232 | tf_op jit(solution)/shard_map/reduce_scatter | solution.py:338
  258.8 1.7 fusion.9
  (7 shorter events, 0.0 us)
Async XLA Ops:
  6.5 200.2 %copy-start = (bf16[768,1536]{1,0:T(8,128)(2,1)S(1)}, bf16[768,1536]{1,0:T(8,128)(2,1)}, u32[]{:S(2)}) copy-start(bf16[768,1536]{1,0:T(8,128)(2,1)} %param.23) | copy-start | bytes 7077892
  6.5 213.6 %reduce-scatter.3.cloned.1.call-start = ((), (), s32[]{:S(2)}) async-start(), calls=%async_computation.2 | async-start | bytes 1179648 | tf_op jit(solution)/shard_map/reduce_scatter | solution.py:332
  14.0 6.6 %copy-start.3 = (bf16[1536,768]{1,0:T(8,128)(2,1)S(1)}, bf16[1536,768]{1,0:T(8,128)(2,1)}, u32[]{:S(2)}) copy-start(bf16[1536,768]{1,0:T(8,128)(2,1)} %param.20) | copy-start | bytes 7077892
  20.6 2.4 copy-start.1
  20.6 2.4 copy-start.2
  23.0 185.1 %copy-start.5 = (bf16[1536]{0:T(1024)(128)(2,1)S(1)}, bf16[1536]{0:T(1024)(128)(2,1)}, u32[]{:S(2)}) copy-start(bf16[1536]{0:T(1024)(128)(2,1)} %param.24) | copy-start | bytes 9220
  23.0 197.1 %copy-start.4 = (bf16[64,1536]{1,0:T(8,128)(2,1)S(1)}, bf16[64,1536]{1,0:T(8,128)(2,1)}, u32[]{:S(2)}) copy-start(bf16[64,1536]{1,0:T(8,128)(2,1)} %param.14) | copy-start | bytes 589828
  208.1 50.7 %reduce-scatter.5.cloned.1.call-start = ((), (), s32[]{:S(2)}) async-start(), calls=%async_computation.3 | async-start | bytes 1179648 | tf_op jit(solution)/shard_map/reduce_scatter | solution.py:338
Sparse Core Ops, SparseCore 0:
  208.2 11.8 reduce-scatter.2
  246.6 12.1 reduce-scatter.4
